TPU v7x, 32 devices: a whole 2x2x4 slice. The times are simulated.
32 devices in a mesh: groups: 2 (over x), row: 16 (over z, y, core), col: 1.
Axes of the slice: x: 2, y: 2, z: 4, core: 2. Of those that a mesh axis runs over, the one named last changes fastest.
Arguments:
- pair_rep: bfloat16 [256, 128, 128], P(('groups', 'row'), 'col'), parts along dimension 0, may hold values from -6 to 6
- residue_mask: int32 [256], P('groups'), parts along dimension 0, may hold values 0 or 1
- crop_length: int32 [2], P('groups'), parts along dimension 0, may hold values from 64 to 128
- norm_gain: float32 [2, 128], replicated, may hold values from 0.25 to 1.75
- mult_proj: bfloat16 [2, 128, 640], replicated, may hold values from -0.5 to 0.5
- mixed_gain: float32 [2, 128], replicated, may hold values from 0.25 to 1.75
- mult_out: bfloat16 [2, 128, 128], replicated, may hold values from -0.5 to 0.5
- att_gain: float32 [128], replicated, may hold values from 0.25 to 1.75
- att_proj: bfloat16 [128, 512], replicated, may hold values from -5 to 5
- att_bias: bfloat16 [128, 4], replicated, may hold values from -0.5 to 0.5
- att_out: bfloat16 [128, 128], replicated, may hold values from -0.5 to 0.5
Outputs:
- pair_out: bfloat16 [256, 128, 128], P(('groups', 'row'), 'col'), parts along dimension 0
There are 2 independent parts, one for each index of `groups`. A program takes and returns all parts, laid end to end along the dimension named above; an argument that names none is the same for every part. Nothing has to cross between parts.
All inputs are finite; a program needn't handle non-finite values.
Results may differ from a plain program's by a relative error of at most 0.03.
Values may be sent and summed in bfloat16 or wider, within the bound.
A program may use at most 64 MiB of HBM per device.

v0:
```python
import functools

import jax
import jax.numpy as jnp
from jax import lax
from jax.experimental import pallas as pl
from jax.experimental.pallas import tpu as pltpu
from jax.sharding import PartitionSpec as P

HID = 128
HEADS = 4
HEAD_DIM = 32
ATT = 128


EPSILON = 1e-05


def normalize(values, gain_vec, along):
    average = jnp.mean(values, axis=along, keepdims=True)
    centered = values - average
    variance = jnp.mean(centered * centered, axis=along, keepdims=True)
    return centered * lax.rsqrt(variance + EPSILON) * gain_vec


def outgoing_product(left_half, right_half):
    return lax.dot_general(
        left_half,
        lax.all_gather(right_half, "row", axis=1, tiled=True),
        (((2,), (2,)), ((0,), (0,))),
        preferred_element_type=jnp.float32,
    )


def incoming_product(left_half, right_half):
    left_cols, right_cols = (
        lax.all_to_all(left_half, "row", split_axis=2, concat_axis=1, tiled=True),
        lax.all_to_all(right_half, "row", split_axis=2, concat_axis=1, tiled=True),
    )
    return lax.dot_general(
        left_cols,
        lax.all_gather(right_cols, "row", axis=2, tiled=True),
        (((1,), (1,)), ((0,), (0,))),
        preferred_element_type=jnp.float32,
    )


def triangle_update(pair_rep, gain_vec, proj_w, out_gain, out_w, pair_mask, incoming):
    normed = normalize(pair_rep.astype(jnp.float32), gain_vec, 2).astype(jnp.bfloat16)
    channels = jnp.einsum(
        "ijd,de->eij", normed, proj_w[:, : 4 * HID], preferred_element_type=jnp.float32
    )
    gate_lin = jnp.einsum(
        "ijd,de->ije", normed, proj_w[:, 4 * HID :], preferred_element_type=jnp.float32
    )
    masked = pair_mask[None, :, :]
    left_proj = (masked * jax.nn.sigmoid(channels[HID : 2 * HID]) * channels[:HID]).astype(
        jnp.bfloat16
    )
    right_proj = (
        masked * jax.nn.sigmoid(channels[3 * HID : 4 * HID]) * channels[2 * HID : 3 * HID]
    ).astype(jnp.bfloat16)
    left_half, right_half = (
        lax.all_to_all(left_proj, "col", split_axis=0, concat_axis=2, tiled=True),
        lax.all_to_all(right_proj, "col", split_axis=0, concat_axis=2, tiled=True),
    )
    if incoming:
        product = incoming_product(left_half, right_half)
    else:
        product = outgoing_product(left_half, right_half)
    mixed = product.astype(jnp.bfloat16)
    mixed_tile = lax.all_to_all(mixed, "col", split_axis=2, concat_axis=0, tiled=True)
    mixed_norm = normalize(mixed_tile.astype(jnp.float32), out_gain[:, None, None], 0).astype(
        jnp.bfloat16
    )
    update = jnp.einsum("cij,cd->ijd", mixed_norm, out_w, preferred_element_type=jnp.float32)
    return (pair_rep.astype(jnp.float32) + jax.nn.sigmoid(gate_lin) * update).astype(jnp.bfloat16)


def local(
    pair_rep,
    residue_mask,
    crop_length,
    norm_gain,
    mult_proj,
    mixed_gain,
    mult_out,
    att_gain,
    att_proj,
    att_bias,
    att_out,
):
    row_count = pair_rep.shape[0]
    col_count = pair_rep.shape[1]
    row_start = lax.axis_index("row") * row_count
    col_start = lax.axis_index("col") * col_count
    positions = jnp.arange(residue_mask.shape[0], dtype=jnp.int32)
    alive = (((residue_mask == 1) | (positions == 0)) & (positions < crop_length[0])).astype(
        jnp.float32
    )
    row_alive = lax.dynamic_slice_in_dim(alive, row_start, row_count, 0)
    col_alive = lax.dynamic_slice_in_dim(alive, col_start, col_count, 0)
    pair_mask = row_alive[:, None] * col_alive[None, :]
    first = triangle_update(
        pair_rep, norm_gain[0], mult_proj[0], mixed_gain[0], mult_out[0], pair_mask, False
    )
    second = triangle_update(
        first, norm_gain[1], mult_proj[1], mixed_gain[1], mult_out[1], pair_mask, True
    )
    normed = normalize(second.astype(jnp.float32), att_gain, 2).astype(jnp.bfloat16)
    projected = jnp.einsum("ijd,de->ije", normed, att_proj, preferred_element_type=jnp.float32)
    queries = projected[..., :ATT].astype(jnp.bfloat16)
    key_rows = projected[..., ATT : 2 * ATT].astype(jnp.bfloat16)
    value_rows = projected[..., 2 * ATT : 3 * ATT].astype(jnp.bfloat16)
    gates = projected[..., 3 * ATT :].astype(jnp.bfloat16)
    bias_tile = jnp.einsum(
        "ijd,dh->hij", normed, att_bias, preferred_element_type=jnp.float32
    ).astype(jnp.bfloat16)
    key_all, value_all, bias_cols = (
        lax.all_gather(key_rows, "col", axis=1, tiled=True),
        lax.all_gather(value_rows, "col", axis=1, tiled=True),
        lax.all_gather(bias_tile, "col", axis=2, tiled=True),
    )
    bias_full = lax.all_gather(bias_cols, "row", axis=1, tiled=True)
    bias_mine = lax.dynamic_slice_in_dim(bias_full, col_start, col_count, 1).astype(jnp.float32)
    total = key_all.shape[1]
    key_mask = jnp.where(alive > 0, 0.0, -1000000000.0).astype(jnp.float32)
    scaling = 1.0 / float(HEAD_DIM) ** 0.5
    query_heads = queries.reshape(row_count, col_count, HEADS, HEAD_DIM)
    key_heads = key_all.reshape(row_count, total, HEADS, HEAD_DIM)
    value_heads = value_all.reshape(row_count, total, HEADS, HEAD_DIM)
    scores = jnp.einsum(
        "ijhd,ikhd->hijk", query_heads, key_heads, preferred_element_type=jnp.float32
    )
    scores = scores * scaling + bias_mine[:, None, :, :] + key_mask[None, None, None, :]
    weights = jax.nn.softmax(scores, axis=-1).astype(jnp.bfloat16)
    attended = jnp.einsum(
        "hijk,ikhd->ijhd", weights, value_heads, preferred_element_type=jnp.float32
    )
    attended = attended.reshape(row_count, col_count, ATT)
    gated = (jax.nn.sigmoid(gates.astype(jnp.float32)) * attended).astype(jnp.bfloat16)
    result = jnp.einsum("ija,ad->ijd", gated, att_out, preferred_element_type=jnp.float32)
    return (second.astype(jnp.float32) + result).astype(jnp.bfloat16)


MESH = pl.DeviceIdType.MESH
BF16 = jnp.bfloat16
F32 = jnp.float32
GROUP = 8
PARTS = 1


def sigmoid(x):
    return 0.5 * jnp.tanh(0.5 * x) + 0.5


def normalize_t(values, gain_col):
    average = jnp.mean(values, axis=0, keepdims=True)
    centered = values - average
    variance = jnp.mean(centered * centered, axis=0, keepdims=True)
    return centered * lax.rsqrt(variance + EPSILON) * gain_col


def mm(a, b, dims=((1,), (0,))):
    return lax.dot_general(a, b, (dims, ((), ())), preferred_element_type=F32)


def fused_kernel(
    n,
    pair_ref,
    mask_ref,
    crop_ref,
    gain_ref,
    proj_ref,
    mgain_ref,
    mout_ref,
    again_ref,
    aproj_ref,
    abias_ref,
    aout_ref,
    out_ref,
    zt,
    og,
    f_left,
    f_right,
    fx_left,
    fx_right,
    f_prod,
    f_bias,
    b_pad,
    b_full,
    kmat,
    qvg,
    proj_t,
    out_t,
    gain_cols,
    qvg_t,
    send_lr,
    recv_lr,
    send_p,
    recv_p,
    send_b,
    recv_b,
    send_sem,
    recv_sem,
):
    me = lax.axis_index("row")
    rows, cols, chans = pair_ref.shape
    mine = chans // n
    block = rows * mine
    half = rows // PARTS
    hblock = half * mine
    heads = abias_ref.shape[0]
    att = chans
    hid = chans

    barrier = pltpu.get_barrier_semaphore()
    for s in range(1, n):
        pl.semaphore_signal(
            barrier, inc=1, device_id={"row": lax.rem(me + s, n)}, device_id_type=MESH
        )

    def column(row_vec):
        return jnp.transpose(jnp.broadcast_to(row_vec.astype(F32), (chans, row_vec.shape[-1])))

    def flip(mat):
        return jnp.transpose(mat.astype(F32)).astype(BF16)

    lane = lax.broadcasted_iota(jnp.int32, (1, cols), 1)
    alive = jnp.where(
        ((mask_ref[...] == 1) | (lane == 0)) & (lane < crop_ref[0]), 1.0, 0.0
    ).astype(F32)

    def row_mask(i):
        here = jnp.where(lane == me * rows + i, alive, 0.0)
        return jnp.sum(here, axis=1, keepdims=True) * alive

    masks = [row_mask(i) for i in range(rows)]

    def exchange(phase, src, dst, p, slot):
        return pltpu.make_async_remote_copy(
            src_ref=src.at[p],
            dst_ref=dst.at[slot],
            send_sem=send_sem.at[phase, p],
            recv_sem=recv_sem.at[phase, slot],
            device_id={"row": p},
            device_id_type=MESH,
        )

    def send_all(phase, src, dst):
        for s in range(n - 1, 0, -1):
            exchange(phase, src, dst, lax.rem(me + s, n), me).start()

    def take_all(phase, src, dst):
        for s in range(1, n):
            q = lax.rem(me + n - s, n)
            exchange(phase, src, dst, q, q).wait_recv()

    def at_row(i):
        return slice(i * cols, (i + 1) * cols)

    def lr_phase(u, k):
        return u * 2 * PARTS + k

    def p_phase(u, k):
        return u * 2 * PARTS + PARTS + k

    def b_phase(k):
        return 4 * PARTS + k

    def project(u, k):
        for i in range(k * half, (k + 1) * half):
            normed = normalize_t(zt[:, at_row(i)].astype(F32), gain_cols[u]).astype(BF16)
            pr = mm(proj_t[u], normed)
            left = masks[i] * sigmoid(pr[hid : 2 * hid]) * pr[:hid]
            right = masks[i] * sigmoid(pr[3 * hid : 4 * hid]) * pr[2 * hid : 3 * hid]
            f_left[:, i] = left.reshape(n, mine, cols)
            f_right[:, i] = right.reshape(n, mine, cols)
            og[:, at_row(i)] = sigmoid(pr[4 * hid :])
        src, dst = send_lr.at[u, k], recv_lr.at[u, k]
        for p in range(n):
            at = slice(k * half, (k + 1) * half)
            src[p, 0] = f_left[p, at].reshape(hblock, cols).astype(BF16)
            src[p, 1] = f_right[p, at].reshape(hblock, cols).astype(BF16)
        if u == 0 and k == 0:
            pl.semaphore_wait(barrier, n - 1)
        send_all(lr_phase(u, k), src, dst)
        dst[me] = src[me]

    def multiply(u):
        for k in range(PARTS):
            src, dst = send_lr.at[u, k], recv_lr.at[u, k]
            take_all(lr_phase(u, k), src, dst)
            for q in range(n):
                at = pl.ds(q * block + k * hblock, hblock)
                fx_left[at, :] = dst[q, 0].astype(F32)
                fx_right[at, :] = dst[q, 1].astype(F32)
        for c in range(mine):
            at = pl.ds(c, n * rows, stride=mine)
            a = fx_left[at, :].astype(BF16)
            b = fx_right[at, :].astype(BF16)
            if u == 0:
                f_prod[at, :] = mm(a, b, ((1,), (1,)))
            else:
                f_prod[at, :] = mm(a, b, ((0,), (0,)))
        for k in range(PARTS):
            src, dst = send_p.at[u, k], recv_p.at[u, k]
            for p in range(n):
                src[p] = f_prod[pl.ds(p * block + k * hblock, hblock), :].astype(BF16)
            send_all(p_phase(u, k), src, dst)
            dst[me] = src[me]

    def finish(u, k):
        src, dst = send_p.at[u, k], recv_p.at[u, k]
        take_all(p_phase(u, k), src, dst)
        for q in range(n):
            f_left[q, k * half : (k + 1) * half] = dst[q].astype(F32).reshape(half, mine, cols)
        for i in range(k * half, (k + 1) * half):
            at = at_row(i)
            mixed = f_left[:, i].reshape(chans, cols)
            mixed_norm = normalize_t(mixed, gain_cols[2 + u]).astype(BF16)
            zt[:, at] = (zt[:, at].astype(F32) + og[:, at] * mm(out_t[u], mixed_norm)).astype(BF16)

    def bias_copy(k, p, slot):
        return pltpu.make_async_remote_copy(
            src_ref=send_b.at[k],
            dst_ref=recv_b.at[k, slot],
            send_sem=send_sem.at[b_phase(k), p],
            recv_sem=recv_sem.at[b_phase(k), slot],
            device_id={"row": p},
            device_id_type=MESH,
        )

    def attention_inputs(k):
        normed_rows = []
        for i in range(k * half, (k + 1) * half):
            normed = normalize_t(zt[:, at_row(i)].astype(F32), gain_cols[4]).astype(BF16)
            normed_rows.append(normed)
            bias_row = mm(b_pad[...].astype(BF16), normed)
            for h in range(heads):
                f_bias[k, h * half + i - k * half : h * half + i - k * half + 1, :] = bias_row[h : h + 1, :]
        send_b[k] = f_bias[k].astype(BF16)
        for s in range(1, n):
            bias_copy(k, lax.rem(me + s, n), me).start()
        recv_b[k, me] = f_bias[k].astype(BF16)
        for i in range(k * half, (k + 1) * half):
            normed = normed_rows[i - k * half]
            kmat[i] = mm(flip(normed), aproj_ref[:, att : 2 * att]).astype(BF16)
            qvg[i] = mm(qvg_t[...], normed).astype(BF16)

    gain_cols[0] = column(gain_ref[0:1, :])
    proj_t[0] = flip(proj_ref[0])
    for i in range(rows):
        zt[:, at_row(i)] = flip(pair_ref[i])
    for k in range(PARTS):
        project(0, k)
    gain_cols[1] = column(gain_ref[1:2, :])
    gain_cols[2] = column(mgain_ref[0:1, :])
    gain_cols[3] = column(mgain_ref[1:2, :])
    gain_cols[4] = column(again_ref[...])
    proj_t[1] = flip(proj_ref[1])
    for u in range(2):
        out_t[u] = flip(mout_ref[u])
    out_t[2] = flip(aout_ref[...])
    qvg_t[:att] = flip(aproj_ref[:, :att])
    qvg_t[att:] = flip(aproj_ref[:, 2 * att :])
    b_pad[...] = jnp.zeros_like(b_pad)
    b_pad[:heads] = abias_ref[...].astype(F32)
    key_mask = column(jnp.where(alive > 0, 0.0, -1000000000.0))
    multiply(0)
    for k in range(PARTS):
        finish(0, k)
        project(1, k)
    multiply(1)
    for k in range(PARTS):
        finish(1, k)
        attention_inputs(k)

    for k in range(PARTS):
        for s in range(1, n):
            q = lax.rem(me + n - s, n)
            bias_copy(k, q, q).wait_recv()
    for h in range(heads):
        pieces = []
        for q in range(n):
            for k in range(PARTS):
                pieces.append(recv_b[k, q].astype(F32)[h * half : (h + 1) * half])
        b_full[h] = jnp.transpose(jnp.concatenate(pieces, axis=0)) + key_mask
    dim = att // heads
    scaling = 1.0 / float(dim) ** 0.5

    def attend(i, carry):
        parts = []
        for h in range(heads):
            ch = slice(h * dim, (h + 1) * dim)
            scores = mm(kmat[i, :, ch], qvg[i, ch, :]) * scaling + b_full[h]
            top = jnp.max(scores, axis=0, keepdims=True)
            e = jnp.exp(scores - top)
            w = (e * (1.0 / jnp.sum(e, axis=0, keepdims=True))).astype(BF16)
            parts.append(mm(qvg[i, att + h * dim : att + (h + 1) * dim, :], w))
        attended = jnp.concatenate(parts, axis=0)
        gated = (sigmoid(qvg[i, 2 * att :, :].astype(F32)) * attended).astype(BF16)
        result = mm(out_t[2], gated)
        at = pl.ds(pl.multiple_of(i * cols, cols), cols)
        out_ref[i] = jnp.transpose(zt[:, at].astype(F32) + result).astype(BF16)
        return carry

    lax.fori_loop(0, rows, attend, 0, unroll=4)

    def drain(s, carry):
        p = lax.rem(me + s, n)
        for k in range(PARTS):
            for u in range(2):
                exchange(lr_phase(u, k), send_lr.at[u, k], recv_lr.at[u, k], p, me).wait_send()
                exchange(p_phase(u, k), send_p.at[u, k], recv_p.at[u, k], p, me).wait_send()
            bias_copy(k, p, me).wait_send()
        return carry

    lax.fori_loop(1, n, drain, 0)


def fused(n, pair_rep, residue_mask, crop_length, norm_gain, mult_proj, mixed_gain, mult_out,
          att_gain, att_proj, att_bias, att_out):
    rows, cols, chans = pair_rep.shape
    heads = att_bias.shape[1]
    mine = chans // n
    block = rows * mine
    hblock = block // PARTS
    vm = pl.BlockSpec(memory_space=pltpu.VMEM)
    sm = pl.BlockSpec(memory_space=pltpu.SMEM)
    big = n * block
    return pl.pallas_call(
        functools.partial(fused_kernel, n),
        out_shape=jax.ShapeDtypeStruct(pair_rep.shape, BF16),
        in_specs=[vm, vm, sm] + [vm] * 8,
        out_specs=vm,
        scratch_shapes=[
            pltpu.VMEM((chans, rows * cols), BF16),
            pltpu.VMEM((chans, rows * cols), F32),
            pltpu.VMEM((n, rows, mine, cols), F32),
            pltpu.VMEM((n, rows, mine, cols), F32),
            pltpu.VMEM((big, cols), F32),
            pltpu.VMEM((big, cols), F32),
            pltpu.VMEM((big, cols), F32),
            pltpu.VMEM((PARTS, heads * rows // PARTS, cols), F32),
            pltpu.VMEM((2 * GROUP, chans), F32),
            pltpu.VMEM((heads, cols, cols), F32),
            pltpu.VMEM((rows, cols, chans), BF16),
            pltpu.VMEM((rows, 3 * chans, cols), BF16),
            pltpu.VMEM((2, mult_proj.shape[2], chans), BF16),
            pltpu.VMEM((3, chans, chans), BF16),
            pltpu.VMEM((5, chans, cols), F32),
            pltpu.VMEM((3 * chans, chans), BF16),
            pltpu.VMEM((2, PARTS, n, 2, hblock, cols), BF16),
            pltpu.VMEM((2, PARTS, n, 2, hblock, cols), BF16),
            pltpu.VMEM((2, PARTS, n, hblock, cols), BF16),
            pltpu.VMEM((2, PARTS, n, hblock, cols), BF16),
            pltpu.VMEM((PARTS, heads * rows // PARTS, cols), BF16),
            pltpu.VMEM((PARTS, n, heads * rows // PARTS, cols), BF16),
            pltpu.SemaphoreType.DMA((5 * PARTS, n)),
            pltpu.SemaphoreType.DMA((5 * PARTS, n)),
        ],
        compiler_params=pltpu.CompilerParams(
            collective_id=0, has_side_effects=True, vmem_limit_bytes=48 * 1024 * 1024
        ),
        name="fused_pair",
    )(
        pair_rep,
        residue_mask.reshape(1, -1),
        crop_length,
        norm_gain,
        mult_proj,
        mixed_gain,
        mult_out,
        att_gain.reshape(1, -1),
        att_proj,
        att_bias.T,
        att_out,
    )


def choose(mesh):
    n = mesh.shape["row"]

    def body(pair_rep, *rest):
        rows, cols, chans = pair_rep.shape
        fits = (
            mesh.shape["col"] == 1
            and chans == n * GROUP
            and rows == GROUP
            and cols == n * rows
            and cols == chans
        )
        if fits:
            return fused(n, pair_rep, *rest)
        return local(pair_rep, *rest)

    return body


def solution(mesh):
    placed = (
        P(("groups", "row"), "col", None),
        P("groups"),
        P("groups"),
        P(),
        P(),
        P(),
        P(),
        P(),
        P(),
        P(),
        P(),
    )
    return jax.shard_map(
        choose(mesh),
        mesh=mesh,
        in_specs=placed,
        out_specs=P(("groups", "row"), "col", None),
        check_vma=False,
    )
```

profile of v0, /device:TPU:0, one launch (start us, length us, event | category | flops | bytes accessed | tf_op | source)
XLA Modules:
  0.0 61.4 jit_solution(15498423610603264452)
XLA Ops:
  0.7 0.0 copy-start.9
  0.7 0.0 copy-start.6
  0.7 0.0 copy-start.7
  0.7 0.0 copy-start.5
  0.7 0.0 copy-start.8
  0.7 0.6 copy-done.9
  1.3 0.0 copy-done.6
  1.3 0.0 copy-done.7
  1.4 0.0 copy-done.5
  1.4 0.0 copy-done.8
  1.4 0.0 copy-start
  1.4 1.0 %copy-done = bf16[2,128,640]{2,1,0:T(8,128)(2,1)S(1)} copy-done((bf16[2,128,640]{2,1,0:T(8,128)(2,1)S(1)}, bf16[2,128,640]{2,1,0:T(8,128)(2,1)}, u32[]{:S(2)}) %copy-start) | copy-done | bytes 327704
  2.4 0.0 copy-start.1
  2.4 0.9 %copy-done.1 = bf16[8,128,128]{2,1,0:T(8,128)(2,1)S(1)} copy-done((bf16[8,128,128]{2,1,0:T(8,128)(2,1)S(1)}, bf16[8,128,128]{2,1,0:T(8,128)(2,1)}, u32[]{:S(2)}) %copy-start.1) | copy-done | bytes 262168
  3.3 0.0 copy-start.2
  3.3 0.9 %copy-done.2 = bf16[128,512]{1,0:T(8,128)(2,1)S(1)} copy-done((bf16[128,512]{1,0:T(8,128)(2,1)S(1)}, bf16[128,512]{1,0:T(8,128)(2,1)}, u32[]{:S(2)}) %copy-start.2) | copy-done | bytes 131096
  4.2 0.0 copy-start.3
  4.2 0.8 %copy-done.3 = bf16[2,128,128]{2,1,0:T(8,128)(2,1)S(1)} copy-done((bf16[2,128,128]{2,1,0:T(8,128)(2,1)S(1)}, bf16[2,128,128]{2,1,0:T(8,128)(2,1)}, u32[]{:S(2)}) %copy-start.3) | copy-done | bytes 65560
  5.1 0.0 copy-start.4
  5.1 0.8 %copy-done.4 = bf16[128,128]{1,0:T(8,128)(2,1)S(1)} copy-done((bf16[128,128]{1,0:T(8,128)(2,1)S(1)}, bf16[128,128]{1,0:T(8,128)(2,1)}, u32[]{:S(2)}) %copy-start.4) | copy-done | bytes 32792
  5.8 54.9 %fused_pair.1 = bf16[8,128,128]{2,1,0:T(8,128)(2,1)S(1)} custom-call(bf16[8,128,128]{2,1,0:T(8,128)(2,1)S(1)} %copy-done.1, s32[1,128]{1,0:T(1,128)S(1)} %bitcast.4, s32[1]{0:T(128)S(6)} %copy.13.crop_ref, f32[2,128]{1,0:T(2,128)S(1)} %copy-done.5, bf16[2,128,640]{2,1,0:T(8,128)(2,1)S(1)} %copy-done, f32[2,128]{1,0:T(2,128)S(1)} %copy-done.6, ...), custom_call_target="tpu_custom_call" | custom-call | tf_op jit(solution)/shard_map/fused_pair/pallas_call | solution.py:432
  60.7 0.7 %copy.14 = bf16[8,128,128]{2,1,0:T(8,128)(2,1)} copy(bf16[8,128,128]{2,1,0:T(8,128)(2,1)S(1)} %fused_pair.1) | data formatting | bytes 524288
Async XLA Ops:
  0.7 0.7 %copy-start.9 = (f32[128]{0:T(128)S(1)}, f32[128]{0:T(128)}, u32[]{:S(2)}) copy-start(f32[128]{0:T(128)} %param.18) | copy-start | bytes 1540
  0.7 0.7 %copy-start.6 = (f32[2,128]{1,0:T(2,128)S(1)}, f32[2,128]{1,0:T(2,128)}, u32[]{:S(2)}) copy-start(f32[2,128]{1,0:T(2,128)} %mgain_ref.1) | copy-start | bytes 3076
  0.7 0.7 %copy-start.7 = (bf16[128,4]{0,1:T(4,128)(2,1)S(1)}, bf16[128,4]{0,1:T(4,128)(2,1)}, u32[]{:S(2)}) copy-start(bf16[128,4]{0,1:T(4,128)(2,1)} %param.20) | copy-start | bytes 3076
  0.7 0.7 %copy-start.5 = (f32[2,128]{1,0:T(2,128)S(1)}, f32[2,128]{1,0:T(2,128)}, u32[]{:S(2)}) copy-start(f32[2,128]{1,0:T(2,128)} %gain_ref.1) | copy-start | bytes 3076
  0.7 0.7 %copy-start.8 = (s32[128]{0:T(128)S(1)}, s32[128]{0:T(128)}, u32[]{:S(2)}) copy-start(s32[128]{0:T(128)} %param.12) | copy-start | bytes 1540
  1.4 1.0 %copy-start = (bf16[2,128,640]{2,1,0:T(8,128)(2,1)S(1)}, bf16[2,128,640]{2,1,0:T(8,128)(2,1)}, u32[]{:S(2)}) copy-start(bf16[2,128,640]{2,1,0:T(8,128)(2,1)} %proj_ref.1) | copy-start | bytes 983044
  2.4 0.9 %copy-start.1 = (bf16[8,128,128]{2,1,0:T(8,128)(2,1)S(1)}, bf16[8,128,128]{2,1,0:T(8,128)(2,1)}, u32[]{:S(2)}) copy-start(bf16[8,128,128]{2,1,0:T(8,128)(2,1)} %pair_ref.1) | copy-start | bytes 786436
  3.3 0.9 %copy-start.2 = (bf16[128,512]{1,0:T(8,128)(2,1)S(1)}, bf16[128,512]{1,0:T(8,128)(2,1)}, u32[]{:S(2)}) copy-start(bf16[128,512]{1,0:T(8,128)(2,1)} %aproj_ref.1) | copy-start | bytes 393220
  4.2 0.8 %copy-start.3 = (bf16[2,128,128]{2,1,0:T(8,128)(2,1)S(1)}, bf16[2,128,128]{2,1,0:T(8,128)(2,1)}, u32[]{:S(2)}) copy-start(bf16[2,128,128]{2,1,0:T(8,128)(2,1)} %mout_ref.1) | copy-start | bytes 196612
  5.1 0.8 %copy-start.4 = (bf16[128,128]{1,0:T(8,128)(2,1)S(1)}, bf16[128,128]{1,0:T(8,128)(2,1)}, u32[]{:S(2)}) copy-start(bf16[128,128]{1,0:T(8,128)(2,1)} %aout_ref.1) | copy-start | bytes 98308
where the time goes:
time: 61.8 us; the launch traced here: 61.4 us
  Pallas kernels  54.9 us (89%)
  local copies, waits for them, and re-layouts  5.82 us (9%)
  between operations  0.71 us (1%)
    pallas_call x1, Pallas kernels, fused(): pl.pallas_call(functools.partial(fused_kernel, n), out_shape=jax.ShapeDty...  54.9 us
    unnamed x21, local copies, waits for them, and re-layouts  5.82 us

commit v1 on v0

--- a/solution.py
+++ b/solution.py
@@ -248,7 +248,7 @@
         )
 
     def send_all(phase, src, dst):
-        for s in range(n - 1, 0, -1):
+        for s in range(1, n):
             exchange(phase, src, dst, lax.rem(me + s, n), me).start()
 
     def take_all(phase, src, dst):

time: 61.8 us -> 64.9 us (1.050)
  Pallas kernels: 54.9 us -> 58.1 us
    pallas_call x1, Pallas kernels: 54.9 us -> 58.1 us  [fused(): pl.pallas_call(functools.partial(fused_kernel, n), out_shape=jax.ShapeDty...]
where the time goes in v1:
time: 64.9 us; the launch traced here: 64.6 us
  Pallas kernels  58.1 us (90%)
  local copies, waits for them, and re-layouts  5.82 us (9%)
  between operations  0.71 us (1%)
    pallas_call x1, Pallas kernels, fused(): pl.pallas_call(functools.partial(fused_kernel, n), out_shape=jax.ShapeDty...  58.1 us
    unnamed x21, local copies, waits for them, and re-layouts  5.82 us

profile of v1, /device:TPU:0, one launch (start us, length us, event | category | flops | bytes accessed | tf_op | source)
XLA Modules:
  0.0 64.6 jit_solution(14437198551792040147)
XLA Ops:
  0.7 0.0 copy-start.9
  0.7 0.0 copy-start.6
  0.7 0.0 copy-start.7
  0.7 0.0 copy-start.5
  0.7 0.0 copy-start.8
  0.7 0.6 copy-done.9
  1.3 0.0 copy-done.6
  1.3 0.0 copy-done.7
  1.4 0.0 copy-done.5
  1.4 0.0 copy-done.8
  1.4 0.0 copy-start
  1.4 1.0 %copy-done = bf16[2,128,640]{2,1,0:T(8,128)(2,1)S(1)} copy-done((bf16[2,128,640]{2,1,0:T(8,128)(2,1)S(1)}, bf16[2,128,640]{2,1,0:T(8,128)(2,1)}, u32[]{:S(2)}) %copy-start) | copy-done | bytes 327704
  2.4 0.0 copy-start.1
  2.4 0.9 %copy-done.1 = bf16[8,128,128]{2,1,0:T(8,128)(2,1)S(1)} copy-done((bf16[8,128,128]{2,1,0:T(8,128)(2,1)S(1)}, bf16[8,128,128]{2,1,0:T(8,128)(2,1)}, u32[]{:S(2)}) %copy-start.1) | copy-done | bytes 262168
  3.3 0.0 copy-start.2
  3.3 0.9 %copy-done.2 = bf16[128,512]{1,0:T(8,128)(2,1)S(1)} copy-done((bf16[128,512]{1,0:T(8,128)(2,1)S(1)}, bf16[128,512]{1,0:T(8,128)(2,1)}, u32[]{:S(2)}) %copy-start.2) | copy-done | bytes 131096
  4.2 0.0 copy-start.3
  4.2 0.8 %copy-done.3 = bf16[2,128,128]{2,1,0:T(8,128)(2,1)S(1)} copy-done((bf16[2,128,128]{2,1,0:T(8,128)(2,1)S(1)}, bf16[2,128,128]{2,1,0:T(8,128)(2,1)}, u32[]{:S(2)}) %copy-start.3) | copy-done | bytes 65560
  5.1 0.0 copy-start.4
  5.1 0.8 %copy-done.4 = bf16[128,128]{1,0:T(8,128)(2,1)S(1)} copy-done((bf16[128,128]{1,0:T(8,128)(2,1)S(1)}, bf16[128,128]{1,0:T(8,128)(2,1)}, u32[]{:S(2)}) %copy-start.4) | copy-done | bytes 32792
  5.8 58.1 %fused_pair.1 = bf16[8,128,128]{2,1,0:T(8,128)(2,1)S(1)} custom-call(bf16[8,128,128]{2,1,0:T(8,128)(2,1)S(1)} %copy-done.1, s32[1,128]{1,0:T(1,128)S(1)} %bitcast.4, s32[1]{0:T(128)S(6)} %copy.13.crop_ref, f32[2,128]{1,0:T(2,128)S(1)} %copy-done.5, bf16[2,128,640]{2,1,0:T(8,128)(2,1)S(1)} %copy-done, f32[2,128]{1,0:T(2,128)S(1)} %copy-done.6, ...), custom_call_target="tpu_custom_call" | custom-call | tf_op jit(solution)/shard_map/fused_pair/pallas_call | solution.py:432
  63.9 0.7 %copy.14 = bf16[8,128,128]{2,1,0:T(8,128)(2,1)} copy(bf16[8,128,128]{2,1,0:T(8,128)(2,1)S(1)} %fused_pair.1) | data formatting | bytes 524288
Async XLA Ops:
  0.7 0.7 %copy-start.9 = (f32[128]{0:T(128)S(1)}, f32[128]{0:T(128)}, u32[]{:S(2)}) copy-start(f32[128]{0:T(128)} %param.18) | copy-start | bytes 1540
  0.7 0.7 %copy-start.6 = (f32[2,128]{1,0:T(2,128)S(1)}, f32[2,128]{1,0:T(2,128)}, u32[]{:S(2)}) copy-start(f32[2,128]{1,0:T(2,128)} %mgain_ref.1) | copy-start | bytes 3076
  0.7 0.7 %copy-start.7 = (bf16[128,4]{0,1:T(4,128)(2,1)S(1)}, bf16[128,4]{0,1:T(4,128)(2,1)}, u32[]{:S(2)}) copy-start(bf16[128,4]{0,1:T(4,128)(2,1)} %param.20) | copy-start | bytes 3076
  0.7 0.7 %copy-start.5 = (f32[2,128]{1,0:T(2,128)S(1)}, f32[2,128]{1,0:T(2,128)}, u32[]{:S(2)}) copy-start(f32[2,128]{1,0:T(2,128)} %gain_ref.1) | copy-start | bytes 3076
  0.7 0.7 %copy-start.8 = (s32[128]{0:T(128)S(1)}, s32[128]{0:T(128)}, u32[]{:S(2)}) copy-start(s32[128]{0:T(128)} %param.12) | copy-start | bytes 1540
  1.4 1.0 %copy-start = (bf16[2,128,640]{2,1,0:T(8,128)(2,1)S(1)}, bf16[2,128,640]{2,1,0:T(8,128)(2,1)}, u32[]{:S(2)}) copy-start(bf16[2,128,640]{2,1,0:T(8,128)(2,1)} %proj_ref.1) | copy-start | bytes 983044
  2.4 0.9 %copy-start.1 = (bf16[8,128,128]{2,1,0:T(8,128)(2,1)S(1)}, bf16[8,128,128]{2,1,0:T(8,128)(2,1)}, u32[]{:S(2)}) copy-start(bf16[8,128,128]{2,1,0:T(8,128)(2,1)} %pair_ref.1) | copy-start | bytes 786436
  3.3 0.9 %copy-start.2 = (bf16[128,512]{1,0:T(8,128)(2,1)S(1)}, bf16[128,512]{1,0:T(8,128)(2,1)}, u32[]{:S(2)}) copy-start(bf16[128,512]{1,0:T(8,128)(2,1)} %aproj_ref.1) | copy-start | bytes 393220
  4.2 0.8 %copy-start.3 = (bf16[2,128,128]{2,1,0:T(8,128)(2,1)S(1)}, bf16[2,128,128]{2,1,0:T(8,128)(2,1)}, u32[]{:S(2)}) copy-start(bf16[2,128,128]{2,1,0:T(8,128)(2,1)} %mout_ref.1) | copy-start | bytes 196612
  5.1 0.8 %copy-start.4 = (bf16[128,128]{1,0:T(8,128)(2,1)S(1)}, bf16[128,128]{1,0:T(8,128)(2,1)}, u32[]{:S(2)}) copy-start(bf16[128,128]{1,0:T(8,128)(2,1)} %aout_ref.1) | copy-start | bytes 98308

commit v2 on v0

--- a/solution.py
+++ b/solution.py
@@ -167,9 +167,20 @@
 
 def fused_kernel(
     n,
+    pair_hbm,
+    mask_hbm,
+    crop_ref,
+    gain_hbm,
+    proj_hbm,
+    mgain_hbm,
+    mout_hbm,
+    again_hbm,
+    aproj_hbm,
+    abias_hbm,
+    aout_hbm,
+    out_ref,
     pair_ref,
     mask_ref,
-    crop_ref,
     gain_ref,
     proj_ref,
     mgain_ref,
@@ -178,7 +189,7 @@
     aproj_ref,
     abias_ref,
     aout_ref,
-    out_ref,
+    load_sem,
     zt,
     og,
     f_left,
@@ -220,6 +231,28 @@
             barrier, inc=1, device_id={"row": lax.rem(me + s, n)}, device_id_type=MESH
         )
 
+    loads = [
+        pltpu.make_async_copy(src, dst, load_sem.at[at])
+        for at, (src, dst) in enumerate((
+            (mask_hbm, mask_ref),
+            (gain_hbm, gain_ref),
+            (proj_hbm.at[0], proj_ref.at[0]),
+            (pair_hbm, pair_ref),
+            (mgain_hbm, mgain_ref),
+            (proj_hbm.at[1], proj_ref.at[1]),
+            (mout_hbm, mout_ref),
+            (again_hbm, again_ref),
+            (aproj_hbm, aproj_ref),
+            (abias_hbm, abias_ref),
+            (aout_hbm, aout_ref),
+        ))
+    ]
+    for load in loads:
+        load.start()
+    rows, cols, chans = pair_ref.shape
+    for load in loads[:4]:
+        load.wait()
+
     def column(row_vec):
         return jnp.transpose(jnp.broadcast_to(row_vec.astype(F32), (chans, row_vec.shape[-1])))
 
@@ -354,6 +387,8 @@
         zt[:, at_row(i)] = flip(pair_ref[i])
     for k in range(PARTS):
         project(0, k)
+    for load in loads[4:]:
+        load.wait()
     gain_cols[1] = column(gain_ref[1:2, :])
     gain_cols[2] = column(mgain_ref[0:1, :])
     gain_cols[3] = column(mgain_ref[1:2, :])
@@ -427,14 +462,29 @@
     block = rows * mine
     hblock = block // PARTS
     vm = pl.BlockSpec(memory_space=pltpu.VMEM)
-    sm = pl.BlockSpec(memory_space=pltpu.SMEM)
+    hbm = pl.BlockSpec(memory_space=pltpu.HBM)
     big = n * block
+
+    def far(operand):
+        return pltpu.with_memory_space_constraint(operand, pltpu.HBM)
+
     return pl.pallas_call(
         functools.partial(fused_kernel, n),
         out_shape=jax.ShapeDtypeStruct(pair_rep.shape, BF16),
-        in_specs=[vm, vm, sm] + [vm] * 8,
+        in_specs=[hbm, hbm, pl.BlockSpec(memory_space=pltpu.SMEM)] + [hbm] * 8,
         out_specs=vm,
         scratch_shapes=[
+            pltpu.VMEM(pair_rep.shape, BF16),
+            pltpu.VMEM((1, cols), jnp.int32),
+            pltpu.VMEM(norm_gain.shape, F32),
+            pltpu.VMEM(mult_proj.shape, BF16),
+            pltpu.VMEM(mixed_gain.shape, F32),
+            pltpu.VMEM(mult_out.shape, BF16),
+            pltpu.VMEM((1, chans), F32),
+            pltpu.VMEM(att_proj.shape, BF16),
+            pltpu.VMEM((heads, chans), BF16),
+            pltpu.VMEM(att_out.shape, BF16),
+            pltpu.SemaphoreType.DMA((11,)),
             pltpu.VMEM((chans, rows * cols), BF16),
             pltpu.VMEM((chans, rows * cols), F32),
             pltpu.VMEM((n, rows, mine, cols), F32),
@@ -465,17 +515,17 @@
         ),
         name="fused_pair",
     )(
-        pair_rep,
-        residue_mask.reshape(1, -1),
+        far(pair_rep),
+        far(residue_mask.reshape(1, -1)),
         crop_length,
-        norm_gain,
-        mult_proj,
-        mixed_gain,
-        mult_out,
-        att_gain.reshape(1, -1),
-        att_proj,
-        att_bias.T,
-        att_out,
+        far(norm_gain),
+        far(mult_proj),
+        far(mixed_gain),
+        far(mult_out),
+        far(att_gain.reshape(1, -1)),
+        far(att_proj),
+        far(att_bias.T),
+        far(att_out),
     )
 
 

time: 61.8 us -> 56.7 us (0.917)
  local copies, waits for them, and re-layouts: 5.82 us -> 0.71 us
    unnamed x21 -> x1, local copies, waits for them, and re-layouts: 5.82 us -> 0.71 us
where the time goes in v2:
time: 56.7 us; the launch traced here: 56.5 us
  Pallas kernels  55.2 us (97%)
  local copies, waits for them, and re-layouts  0.71 us (1%)
  between operations  0.66 us (1%)
    pallas_call x1, Pallas kernels, fused(): pl.pallas_call(functools.partial(fused_kernel, n), out_shape=jax.ShapeDty...  55.2 us

profile of v2, /device:TPU:0, one launch (start us, length us, event | category | flops | bytes accessed | tf_op | source)
XLA Modules:
  0.0 56.5 jit_solution(10239721723235151426)
XLA Ops:
  0.7 55.2 %fused_pair.1 = bf16[8,128,128]{2,1,0:T(8,128)(2,1)S(1)} custom-call(bf16[8,128,128]{2,1,0:T(8,128)(2,1)} %pair_hbm.1, s32[1,128]{1,0:T(1,128)} %bitcast.4, s32[1]{0:T(128)S(6)} %copy.13.crop_ref, f32[2,128]{1,0:T(2,128)} %gain_hbm.1, bf16[2,128,640]{2,1,0:T(8,128)(2,1)} %proj_hbm.1, f32[2,128]{1,0:T(2,128)} %mgain_hbm.1, bf16[2,128,128]{2,1,0:T(8,128)(2,1)} %mout_hbm.1, ...), custom_call_target="tpu_custom_call" | custom-call | tf_op jit(solution)/shard_map/fused_pair/pallas_call | solution.py:471
  55.8 0.7 %copy.14 = bf16[8,128,128]{2,1,0:T(8,128)(2,1)} copy(bf16[8,128,128]{2,1,0:T(8,128)(2,1)S(1)} %fused_pair.1) | data formatting | bytes 524288

commit v3 on v2

--- a/solution.py
+++ b/solution.py
@@ -147,7 +147,10 @@
 BF16 = jnp.bfloat16
 F32 = jnp.float32
 GROUP = 8
-PARTS = 1
+FIRST = 1
+MIDDLE = 4
+LAST = 2
+LOG2E = 1.4426950408889634
 
 
 def sigmoid(x):
@@ -192,38 +195,45 @@
     load_sem,
     zt,
     og,
-    f_left,
-    f_right,
     fx_left,
     fx_right,
     f_prod,
-    f_bias,
     b_pad,
     b_full,
     kmat,
-    qvg,
+    q_heads,
+    vmat,
+    gmat,
+    scores,
     proj_t,
     out_t,
     gain_cols,
     qvg_t,
-    send_lr,
-    recv_lr,
-    send_p,
-    recv_p,
+    send_a,
+    recv_a,
     send_b,
     recv_b,
+    send_c,
+    recv_c,
+    send_d,
+    recv_d,
+    send_e,
+    recv_e,
     send_sem,
     recv_sem,
 ):
     me = lax.axis_index("row")
     rows, cols, chans = pair_ref.shape
+    peers = n // 2
     mine = chans // n
-    block = rows * mine
-    half = rows // PARTS
-    hblock = half * mine
+    wide = chans // peers
     heads = abias_ref.shape[0]
     att = chans
     hid = chans
+    dim = att // heads
+    here = lax.rem(me, peers)
+    near = me - here
+    far = peers - near
 
     barrier = pltpu.get_barrier_semaphore()
     for s in range(1, n):
@@ -249,7 +259,6 @@
     ]
     for load in loads:
         load.start()
-    rows, cols, chans = pair_ref.shape
     for load in loads[:4]:
         load.wait()
 
@@ -265,128 +274,194 @@
     ).astype(F32)
 
     def row_mask(i):
-        here = jnp.where(lane == me * rows + i, alive, 0.0)
-        return jnp.sum(here, axis=1, keepdims=True) * alive
+        own = jnp.where(lane == me * rows + i, alive, 0.0)
+        return jnp.sum(own, axis=1, keepdims=True) * alive
 
     masks = [row_mask(i) for i in range(rows)]
 
-    def exchange(phase, src, dst, p, slot):
+    def at_row(i):
+        return slice(i * cols, (i + 1) * cols)
+
+    def chunk(k, parts):
+        return range(k * rows // parts, (k + 1) * rows // parts)
+
+    def remote(phase, src, dst, p):
         return pltpu.make_async_remote_copy(
-            src_ref=src.at[p],
-            dst_ref=dst.at[slot],
-            send_sem=send_sem.at[phase, p],
-            recv_sem=recv_sem.at[phase, slot],
+            src_ref=src,
+            dst_ref=dst,
+            send_sem=send_sem.at[phase],
+            recv_sem=recv_sem.at[phase],
             device_id={"row": p},
             device_id_type=MESH,
         )
 
-    def send_all(phase, src, dst):
-        for s in range(n - 1, 0, -1):
-            exchange(phase, src, dst, lax.rem(me + s, n), me).start()
-
-    def take_all(phase, src, dst):
-        for s in range(1, n):
-            q = lax.rem(me + n - s, n)
-            exchange(phase, src, dst, q, q).wait_recv()
-
-    def at_row(i):
-        return slice(i * cols, (i + 1) * cols)
-
-    def lr_phase(u, k):
-        return u * 2 * PARTS + k
-
-    def p_phase(u, k):
-        return u * 2 * PARTS + PARTS + k
-
-    def b_phase(k):
-        return 4 * PARTS + k
-
-    def project(u, k):
-        for i in range(k * half, (k + 1) * half):
-            normed = normalize_t(zt[:, at_row(i)].astype(F32), gain_cols[u]).astype(BF16)
-            pr = mm(proj_t[u], normed)
-            left = masks[i] * sigmoid(pr[hid : 2 * hid]) * pr[:hid]
-            right = masks[i] * sigmoid(pr[3 * hid : 4 * hid]) * pr[2 * hid : 3 * hid]
-            f_left[:, i] = left.reshape(n, mine, cols)
-            f_right[:, i] = right.reshape(n, mine, cols)
-            og[:, at_row(i)] = sigmoid(pr[4 * hid :])
-        src, dst = send_lr.at[u, k], recv_lr.at[u, k]
-        for p in range(n):
-            at = slice(k * half, (k + 1) * half)
-            src[p, 0] = f_left[p, at].reshape(hblock, cols).astype(BF16)
-            src[p, 1] = f_right[p, at].reshape(hblock, cols).astype(BF16)
-        if u == 0 and k == 0:
+    def others():
+        return [lax.rem(me + s, n) for s in range(n - 1, 0, -1)]
+
+    def near_others():
+        return [near + lax.rem(here + s, peers) for s in range(peers - 1, 0, -1)]
+
+    def far_others():
+        return [far + lax.rem(here + s, peers) for s in range(peers - 1, -1, -1)]
+
+    def a_both(k, p):
+        src = send_a.at[k, pl.ds(2 * lax.rem(p, peers), 2)]
+        return remote(k, src, recv_a.at[k, pl.ds(2 * me, 2)], p)
+
+    def a_right(k, p):
+        return remote(k, send_a.at[k, 2 * lax.rem(p, peers) + 1], recv_a.at[k, 2 * me + 1], p)
+
+    def a_all(k):
+        block = recv_a.at[k, : 2 * (peers - 1) + peers]
+        return remote(k, block, block, me)
+
+    def b_copy(k, p):
+        return remote(FIRST + k, send_b.at[k, lax.rem(p, peers)], recv_b.at[k, here], p)
+
+    def b_all(k):
+        return remote(FIRST + k, send_b.at[k, : peers - 1], recv_b.at[k, : peers - 1], me)
+
+    def c_copy(k, p):
+        return remote(FIRST + MIDDLE + k, send_c.at[k, p], recv_c.at[k, me], p)
+
+    def c_all(k):
+        return remote(FIRST + MIDDLE + k, send_c.at[k, : n - 1], recv_c.at[k, : n - 1], me)
+
+    def d_copy(k, p):
+        return remote(FIRST + 2 * MIDDLE + k, send_d.at[k, p], recv_d.at[k, me], p)
+
+    def d_all(k):
+        return remote(FIRST + 2 * MIDDLE + k, send_d.at[k, : n - 1], recv_d.at[k, : n - 1], me)
+
+    def e_copy(k, p):
+        return remote(FIRST + 2 * MIDDLE + LAST + k, send_e.at[k], recv_e.at[k, me], p)
+
+    def e_all(k):
+        block = recv_e.at[k, : n - 1]
+        return remote(FIRST + 2 * MIDDLE + LAST + k, block, block, me)
+
+    def project(u, i):
+        normed = normalize_t(zt[:, at_row(i)].astype(F32), gain_cols[u]).astype(BF16)
+        pr = mm(proj_t[u], normed)
+        left = masks[i] * sigmoid(pr[hid : 2 * hid]) * pr[:hid]
+        right = masks[i] * sigmoid(pr[3 * hid : 4 * hid]) * pr[2 * hid : 3 * hid]
+        og[:, at_row(i)] = sigmoid(pr[4 * hid :])
+        return left, right
+
+    def start_first(k):
+        for r, i in enumerate(chunk(k, FIRST)):
+            for side, half in enumerate(project(0, i)):
+                parts = half.astype(BF16)
+                for p in range(peers):
+                    send_a[k, 2 * p + side, r * wide : (r + 1) * wide] = parts[
+                        p * wide : (p + 1) * wide
+                    ]
+        if k == 0:
             pl.semaphore_wait(barrier, n - 1)
-        send_all(lr_phase(u, k), src, dst)
-        dst[me] = src[me]
-
-    def multiply(u):
-        for k in range(PARTS):
-            src, dst = send_lr.at[u, k], recv_lr.at[u, k]
-            take_all(lr_phase(u, k), src, dst)
+        for p in far_others():
+            a_right(k, p).start()
+        for p in near_others():
+            a_both(k, p).start()
+        recv_a[k, pl.ds(2 * me, 2)] = send_a[k, pl.ds(2 * here, 2)]
+
+    def multiply_first():
+        span = rows // FIRST * wide
+        for k in range(FIRST):
+            a_all(k).wait_recv()
+            for q in range(peers):
+                at = q * rows * wide + k * span
+                fx_left[at : at + span] = recv_a[k, 2 * (near + q)].astype(F32)
             for q in range(n):
-                at = pl.ds(q * block + k * hblock, hblock)
-                fx_left[at, :] = dst[q, 0].astype(F32)
-                fx_right[at, :] = dst[q, 1].astype(F32)
+                at = q * rows * wide + k * span
+                fx_right[at : at + span] = recv_a[k, 2 * q + 1].astype(F32)
+        for c in range(wide):
+            at = pl.ds(c, peers * rows, stride=wide)
+            a = fx_left[at, :].astype(BF16)
+            b = fx_right[pl.ds(c, n * rows, stride=wide), :].astype(BF16)
+            f_prod[at, :] = mm(a, b, ((1,), (1,)))
+        span = rows // MIDDLE * wide
+        for k in range(MIDDLE):
+            for p in range(peers):
+                send_b[k, p] = f_prod[pl.ds(p * rows * wide + k * span, span), :].astype(BF16)
+            for p in near_others():
+                b_copy(k, p).start()
+            recv_b[k, here] = send_b[k, here]
+
+    def finish(u, i, mixed):
+        at = at_row(i)
+        mixed_norm = normalize_t(mixed, gain_cols[2 + u]).astype(BF16)
+        zt[:, at] = (zt[:, at].astype(F32) + og[:, at] * mm(out_t[u], mixed_norm)).astype(BF16)
+
+    def turn(k):
+        b_all(k).wait_recv()
+        halves = ([], [])
+        for r, i in enumerate(chunk(k, MIDDLE)):
+            mixed = recv_b[k, :, r * wide : (r + 1) * wide].reshape(chans, cols).astype(F32)
+            finish(0, i, mixed)
+            for side, half in enumerate(project(1, i)):
+                halves[side].append(half.reshape(n, mine, cols))
+        for side in range(2):
+            send_c[k, :, side] = jnp.concatenate(halves[side], axis=1).astype(BF16)
+        for p in others():
+            c_copy(k, p).start()
+        recv_c[k, me] = send_c[k, me]
+
+    def multiply_second():
+        span = rows // MIDDLE * mine
+        for k in range(MIDDLE):
+            c_all(k).wait_recv()
+            for q in range(n):
+                at = q * rows * mine + k * span
+                fx_left[at : at + span] = recv_c[k, q, 0].astype(F32)
+                fx_right[at : at + span] = recv_c[k, q, 1].astype(F32)
         for c in range(mine):
             at = pl.ds(c, n * rows, stride=mine)
             a = fx_left[at, :].astype(BF16)
             b = fx_right[at, :].astype(BF16)
-            if u == 0:
-                f_prod[at, :] = mm(a, b, ((1,), (1,)))
-            else:
-                f_prod[at, :] = mm(a, b, ((0,), (0,)))
-        for k in range(PARTS):
-            src, dst = send_p.at[u, k], recv_p.at[u, k]
+            f_prod[at, :] = mm(a, b, ((0,), (0,)))
+        span = rows // LAST * mine
+        for k in range(LAST):
             for p in range(n):
-                src[p] = f_prod[pl.ds(p * block + k * hblock, hblock), :].astype(BF16)
-            send_all(p_phase(u, k), src, dst)
-            dst[me] = src[me]
-
-    def finish(u, k):
-        src, dst = send_p.at[u, k], recv_p.at[u, k]
-        take_all(p_phase(u, k), src, dst)
-        for q in range(n):
-            f_left[q, k * half : (k + 1) * half] = dst[q].astype(F32).reshape(half, mine, cols)
-        for i in range(k * half, (k + 1) * half):
-            at = at_row(i)
-            mixed = f_left[:, i].reshape(chans, cols)
-            mixed_norm = normalize_t(mixed, gain_cols[2 + u]).astype(BF16)
-            zt[:, at] = (zt[:, at].astype(F32) + og[:, at] * mm(out_t[u], mixed_norm)).astype(BF16)
-
-    def bias_copy(k, p, slot):
-        return pltpu.make_async_remote_copy(
-            src_ref=send_b.at[k],
-            dst_ref=recv_b.at[k, slot],
-            send_sem=send_sem.at[b_phase(k), p],
-            recv_sem=recv_sem.at[b_phase(k), slot],
-            device_id={"row": p},
-            device_id_type=MESH,
-        )
-
-    def attention_inputs(k):
+                send_d[k, p] = f_prod[pl.ds(p * rows * mine + k * span, span), :].astype(BF16)
+            for p in others():
+                d_copy(k, p).start()
+            recv_d[k, me] = send_d[k, me]
+
+    def close(k):
+        d_all(k).wait_recv()
+        mixed_all = recv_d[k].astype(F32)
+        biases = []
         normed_rows = []
-        for i in range(k * half, (k + 1) * half):
+        for r, i in enumerate(chunk(k, LAST)):
+            finish(1, i, mixed_all[:, r * mine : (r + 1) * mine].reshape(chans, cols))
             normed = normalize_t(zt[:, at_row(i)].astype(F32), gain_cols[4]).astype(BF16)
             normed_rows.append(normed)
-            bias_row = mm(b_pad[...].astype(BF16), normed)
+            biases.append(mm(b_pad[...].astype(BF16), normed))
+        send_e[k] = jnp.concatenate(
+            [row[h : h + 1] for h in range(heads) for row in biases], axis=0
+        ).astype(BF16)
+        for p in others():
+            e_copy(k, p).start()
+        recv_e[k, me] = send_e[k]
+        return normed_rows
+
+    def attention_inputs(k, normed_rows):
+        for i, normed in zip(chunk(k, LAST), normed_rows):
+            kmat[i] = mm(flip(normed), aproj_ref[:, att : 2 * att]).astype(BF16)
+            qvg = mm(qvg_t[...], normed).astype(BF16)
             for h in range(heads):
-                f_bias[k, h * half + i - k * half : h * half + i - k * half + 1, :] = bias_row[h : h + 1, :]
-        send_b[k] = f_bias[k].astype(BF16)
-        for s in range(1, n):
-            bias_copy(k, lax.rem(me + s, n), me).start()
-        recv_b[k, me] = f_bias[k].astype(BF16)
-        for i in range(k * half, (k + 1) * half):
-            normed = normed_rows[i - k * half]
-            kmat[i] = mm(flip(normed), aproj_ref[:, att : 2 * att]).astype(BF16)
-            qvg[i] = mm(qvg_t[...], normed).astype(BF16)
+                ch = slice(h * dim, (h + 1) * dim)
+                q_heads[i, ch, h * cols : (h + 1) * cols] = qvg[ch]
+            vmat[i] = qvg[att : 2 * att]
+            gmat[i] = sigmoid(qvg[2 * att :].astype(F32))
+            scores[i] = mm(kmat[i], q_heads[i]) * (LOG2E / float(dim) ** 0.5)
 
     gain_cols[0] = column(gain_ref[0:1, :])
     proj_t[0] = flip(proj_ref[0])
     for i in range(rows):
         zt[:, at_row(i)] = flip(pair_ref[i])
-    for k in range(PARTS):
-        project(0, k)
+    for k in range(FIRST):
+        start_first(k)
     for load in loads[4:]:
         load.wait()
     gain_cols[1] = column(gain_ref[1:2, :])
@@ -401,40 +476,46 @@
     qvg_t[att:] = flip(aproj_ref[:, 2 * att :])
     b_pad[...] = jnp.zeros_like(b_pad)
     b_pad[:heads] = abias_ref[...].astype(F32)
+    q_heads[...] = jnp.zeros_like(q_heads)
     key_mask = column(jnp.where(alive > 0, 0.0, -1000000000.0))
-    multiply(0)
-    for k in range(PARTS):
-        finish(0, k)
-        project(1, k)
-    multiply(1)
-    for k in range(PARTS):
-        finish(1, k)
-        attention_inputs(k)
-
-    for k in range(PARTS):
-        for s in range(1, n):
-            q = lax.rem(me + n - s, n)
-            bias_copy(k, q, q).wait_recv()
+    multiply_first()
+    for k in range(MIDDLE):
+        turn(k)
+    for k in range(FIRST):
+        a_all(k).wait_send()
+    for k in range(MIDDLE):
+        b_all(k).wait_send()
+    multiply_second()
+    for k in range(MIDDLE):
+        c_all(k).wait_send()
+    closed = [close(k) for k in range(LAST)]
+    for k in range(LAST):
+        attention_inputs(k, closed[k])
+    for k in range(LAST):
+        d_all(k).wait_send()
+
+    for k in range(LAST):
+        e_all(k).wait_recv()
+    part = rows // LAST
     for h in range(heads):
         pieces = []
         for q in range(n):
-            for k in range(PARTS):
-                pieces.append(recv_b[k, q].astype(F32)[h * half : (h + 1) * half])
-        b_full[h] = jnp.transpose(jnp.concatenate(pieces, axis=0)) + key_mask
-    dim = att // heads
-    scaling = 1.0 / float(dim) ** 0.5
+            for k in range(LAST):
+                pieces.append(recv_e[k, q].astype(F32)[h * part : (h + 1) * part])
+        across = jnp.transpose(jnp.concatenate(pieces, axis=0))
+        b_full[:, h * cols : (h + 1) * cols] = (across + key_mask) * LOG2E
 
     def attend(i, carry):
         parts = []
         for h in range(heads):
-            ch = slice(h * dim, (h + 1) * dim)
-            scores = mm(kmat[i, :, ch], qvg[i, ch, :]) * scaling + b_full[h]
-            top = jnp.max(scores, axis=0, keepdims=True)
-            e = jnp.exp(scores - top)
-            w = (e * (1.0 / jnp.sum(e, axis=0, keepdims=True))).astype(BF16)
-            parts.append(mm(qvg[i, att + h * dim : att + (h + 1) * dim, :], w))
+            at = slice(h * cols, (h + 1) * cols)
+            total = scores[i, :, at] + b_full[:, at]
+            e = jnp.exp2(total - jnp.max(total, axis=0, keepdims=True))
+            inverse = 1.0 / jnp.sum(e, axis=0, keepdims=True)
+            w = (e * inverse).astype(BF16)
+            parts.append(mm(vmat[i, h * dim : (h + 1) * dim, :], w))
         attended = jnp.concatenate(parts, axis=0)
-        gated = (sigmoid(qvg[i, 2 * att :, :].astype(F32)) * attended).astype(BF16)
+        gated = (gmat[i] * attended).astype(BF16)
         result = mm(out_t[2], gated)
         at = pl.ds(pl.multiple_of(i * cols, cols), cols)
         out_ref[i] = jnp.transpose(zt[:, at].astype(F32) + result).astype(BF16)
@@ -442,28 +523,27 @@
 
     lax.fori_loop(0, rows, attend, 0, unroll=4)
 
-    def drain(s, carry):
-        p = lax.rem(me + s, n)
-        for k in range(PARTS):
-            for u in range(2):
-                exchange(lr_phase(u, k), send_lr.at[u, k], recv_lr.at[u, k], p, me).wait_send()
-                exchange(p_phase(u, k), send_p.at[u, k], recv_p.at[u, k], p, me).wait_send()
-            bias_copy(k, p, me).wait_send()
-        return carry
-
-    lax.fori_loop(1, n, drain, 0)
+    for k in range(LAST):
+        e_all(k).wait_send()
 
 
 def fused(n, pair_rep, residue_mask, crop_length, norm_gain, mult_proj, mixed_gain, mult_out,
           att_gain, att_proj, att_bias, att_out):
     rows, cols, chans = pair_rep.shape
     heads = att_bias.shape[1]
+    peers = n // 2
     mine = chans // n
-    block = rows * mine
-    hblock = block // PARTS
+    wide = chans // peers
     vm = pl.BlockSpec(memory_space=pltpu.VMEM)
     hbm = pl.BlockSpec(memory_space=pltpu.HBM)
-    big = n * block
+    phases = FIRST + 2 * MIDDLE + 2 * LAST
+    first = pltpu.VMEM((FIRST, 2 * peers, rows // FIRST * wide, cols), BF16)
+    first_in = pltpu.VMEM((FIRST, 2 * n, rows // FIRST * wide, cols), BF16)
+    back = pltpu.VMEM((MIDDLE, peers, rows // MIDDLE * wide, cols), BF16)
+    second = pltpu.VMEM((MIDDLE, n, 2, rows // MIDDLE * mine, cols), BF16)
+    home = pltpu.VMEM((LAST, n, rows // LAST * mine, cols), BF16)
+    bias = pltpu.VMEM((LAST, heads * rows // LAST, cols), BF16)
+    bias_in = pltpu.VMEM((LAST, n, heads * rows // LAST, cols), BF16)
 
     def far(operand):
         return pltpu.with_memory_space_constraint(operand, pltpu.HBM)
@@ -487,28 +567,32 @@
             pltpu.SemaphoreType.DMA((11,)),
             pltpu.VMEM((chans, rows * cols), BF16),
             pltpu.VMEM((chans, rows * cols), F32),
-            pltpu.VMEM((n, rows, mine, cols), F32),
-            pltpu.VMEM((n, rows, mine, cols), F32),
-            pltpu.VMEM((big, cols), F32),
-            pltpu.VMEM((big, cols), F32),
-            pltpu.VMEM((big, cols), F32),
-            pltpu.VMEM((PARTS, heads * rows // PARTS, cols), F32),
+            pltpu.VMEM((n * rows * mine, cols), F32),
+            pltpu.VMEM((n * rows * wide, cols), F32),
+            pltpu.VMEM((n * rows * mine, cols), F32),
             pltpu.VMEM((2 * GROUP, chans), F32),
-            pltpu.VMEM((heads, cols, cols), F32),
+            pltpu.VMEM((cols, heads * cols), F32),
             pltpu.VMEM((rows, cols, chans), BF16),
-            pltpu.VMEM((rows, 3 * chans, cols), BF16),
+            pltpu.VMEM((rows, chans, heads * cols), BF16),
+            pltpu.VMEM((rows, chans, cols), BF16),
+            pltpu.VMEM((rows, chans, cols), F32),
+            pltpu.VMEM((rows, cols, heads * cols), F32),
             pltpu.VMEM((2, mult_proj.shape[2], chans), BF16),
             pltpu.VMEM((3, chans, chans), BF16),
             pltpu.VMEM((5, chans, cols), F32),
             pltpu.VMEM((3 * chans, chans), BF16),
-            pltpu.VMEM((2, PARTS, n, 2, hblock, cols), BF16),
-            pltpu.VMEM((2, PARTS, n, 2, hblock, cols), BF16),
-            pltpu.VMEM((2, PARTS, n, hblock, cols), BF16),
-            pltpu.VMEM((2, PARTS, n, hblock, cols), BF16),
-            pltpu.VMEM((PARTS, heads * rows // PARTS, cols), BF16),
-            pltpu.VMEM((PARTS, n, heads * rows // PARTS, cols), BF16),
-            pltpu.SemaphoreType.DMA((5 * PARTS, n)),
-            pltpu.SemaphoreType.DMA((5 * PARTS, n)),
+            first,
+            first_in,
+            back,
+            back,
+            second,
+            second,
+            home,
+            home,
+            bias,
+            bias_in,
+            pltpu.SemaphoreType.DMA((phases,)),
+            pltpu.SemaphoreType.DMA((phases,)),
         ],
         compiler_params=pltpu.CompilerParams(
             collective_id=0, has_side_effects=True, vmem_limit_bytes=48 * 1024 * 1024
@@ -536,6 +620,7 @@
         rows, cols, chans = pair_rep.shape
         fits = (
             mesh.shape["col"] == 1
+            and n % 2 == 0
             and chans == n * GROUP
             and rows == GROUP
             and cols == n * rows

time: 56.7 us -> 53.8 us (0.949)
  Pallas kernels: 55.2 us -> 52.3 us
    pallas_call x1, Pallas kernels: 55.2 us -> 52.3 us  [fused(): pl.pallas_call(functools.partial(fused_kernel, n), out_shape=jax.ShapeDty...]
where the time goes in v3:
time: 53.8 us; the launch traced here: 53.7 us
  Pallas kernels  52.3 us (97%)
  local copies, waits for them, and re-layouts  0.71 us (1%)
  between operations  0.66 us (1%)
    pallas_call x1, Pallas kernels, fused(): pl.pallas_call(functools.partial(fused_kernel, n), out_shape=jax.ShapeDty...  52.3 us

profile of v3, /device:TPU:0, one launch (start us, length us, event | category | flops | bytes accessed | tf_op | source)
XLA Modules:
  0.0 53.7 jit_solution(11218739974955742421)
XLA Ops:
  0.7 52.3 %fused_pair.1 = bf16[8,128,128]{2,1,0:T(8,128)(2,1)S(1)} custom-call(bf16[8,128,128]{2,1,0:T(8,128)(2,1)} %pair_hbm.1, s32[1,128]{1,0:T(1,128)} %bitcast.4, s32[1]{0:T(128)S(6)} %copy.13.crop_ref, f32[2,128]{1,0:T(2,128)} %gain_hbm.1, bf16[2,128,640]{2,1,0:T(8,128)(2,1)} %proj_hbm.1, f32[2,128]{1,0:T(2,128)} %mgain_hbm.1, bf16[2,128,128]{2,1,0:T(8,128)(2,1)} %mout_hbm.1, ...), custom_call_target="tpu_custom_call" | custom-call | tf_op jit(solution)/shard_map/fused_pair/pallas_call | solution.py:551
  53.0 0.7 %copy.14 = bf16[8,128,128]{2,1,0:T(8,128)(2,1)} copy(bf16[8,128,128]{2,1,0:T(8,128)(2,1)S(1)} %fused_pair.1) | data formatting | bytes 524288

commit v4 on v3

--- a/solution.py
+++ b/solution.py
@@ -149,6 +149,7 @@
 GROUP = 8
 FIRST = 1
 MIDDLE = 4
+SHARED = 2
 LAST = 2
 LOG2E = 1.4426950408889634
 
@@ -215,8 +216,12 @@
     recv_b,
     send_c,
     recv_c,
+    send_f,
+    recv_f,
     send_d,
     recv_d,
+    send_g,
+    recv_g,
     send_e,
     recv_e,
     send_sem,
@@ -234,6 +239,13 @@
     here = lax.rem(me, peers)
     near = me - here
     far = peers - near
+
+    c_phase = FIRST + MIDDLE
+    f_phase = c_phase + MIDDLE
+    d_phase = f_phase + SHARED
+    g_phase = d_phase + LAST
+    e_phase = g_phase + LAST
+    few = mine // 2
 
     barrier = pltpu.get_barrier_semaphore()
     for s in range(1, n):
@@ -295,14 +307,21 @@
             device_id_type=MESH,
         )
 
+    def partner(s):
+        place, at = 1, 0
+        while place < n:
+            bit = lax.rem(lax.div(me, place) + s // place % 2, 2)
+            at, place = at + place * bit, 2 * place
+        return at
+
     def others():
-        return [lax.rem(me + s, n) for s in range(n - 1, 0, -1)]
+        return [partner(s) for s in range(n - 1, 0, -1)]
 
     def near_others():
-        return [near + lax.rem(here + s, peers) for s in range(peers - 1, 0, -1)]
+        return [partner(s) for s in range(peers - 1, 0, -1)]
 
     def far_others():
-        return [far + lax.rem(here + s, peers) for s in range(peers - 1, -1, -1)]
+        return [partner(s) for s in range(n - 1, peers - 1, -1)]
 
     def a_both(k, p):
         src = send_a.at[k, pl.ds(2 * lax.rem(p, peers), 2)]
@@ -322,23 +341,35 @@
         return remote(FIRST + k, send_b.at[k, : peers - 1], recv_b.at[k, : peers - 1], me)
 
     def c_copy(k, p):
-        return remote(FIRST + MIDDLE + k, send_c.at[k, p], recv_c.at[k, me], p)
+        return remote(c_phase + k, send_c.at[k, lax.rem(p, peers)], recv_c.at[k, here], p)
 
     def c_all(k):
-        return remote(FIRST + MIDDLE + k, send_c.at[k, : n - 1], recv_c.at[k, : n - 1], me)
+        return remote(c_phase + k, send_c.at[k, : peers - 1], recv_c.at[k, : peers - 1], me)
+
+    def f_copy(k, p):
+        return remote(f_phase + k, send_f.at[k, p], recv_f.at[k, me], p)
+
+    def f_all(k):
+        return remote(f_phase + k, send_f.at[k, : n - 1], recv_f.at[k, : n - 1], me)
 
     def d_copy(k, p):
-        return remote(FIRST + 2 * MIDDLE + k, send_d.at[k, p], recv_d.at[k, me], p)
+        return remote(d_phase + k, send_d.at[k, p], recv_d.at[k, me], p)
 
     def d_all(k):
-        return remote(FIRST + 2 * MIDDLE + k, send_d.at[k, : n - 1], recv_d.at[k, : n - 1], me)
+        return remote(d_phase + k, send_d.at[k, : n - 1], recv_d.at[k, : n - 1], me)
+
+    def g_copy(k, p):
+        return remote(g_phase + k, send_g.at[k, p], recv_g.at[k, me], p)
+
+    def g_all(k):
+        return remote(g_phase + k, send_g.at[k, : n - 1], recv_g.at[k, : n - 1], me)
 
     def e_copy(k, p):
-        return remote(FIRST + 2 * MIDDLE + LAST + k, send_e.at[k], recv_e.at[k, me], p)
+        return remote(e_phase + k, send_e.at[k], recv_e.at[k, me], p)
 
     def e_all(k):
         block = recv_e.at[k, : n - 1]
-        return remote(FIRST + 2 * MIDDLE + LAST + k, block, block, me)
+        return remote(e_phase + k, block, block, me)
 
     def project(u, i):
         normed = normalize_t(zt[:, at_row(i)].astype(F32), gain_cols[u]).astype(BF16)
@@ -392,6 +423,17 @@
         mixed_norm = normalize_t(mixed, gain_cols[2 + u]).astype(BF16)
         zt[:, at] = (zt[:, at].astype(F32) + og[:, at] * mm(out_t[u], mixed_norm)).astype(BF16)
 
+    low = lax.broadcasted_iota(jnp.int32, (peers * mine, cols), 0) % mine < few
+
+    def trade(x, y):
+        x, y = x.reshape(peers * mine, cols), y.reshape(peers * mine, cols)
+        up = pltpu.roll(x, peers * mine - few, 0)
+        down = pltpu.roll(y, few, 0)
+        pair = jnp.where(low, x, down), jnp.where(low, up, y)
+        return [half.reshape(peers, mine, cols) for half in pair]
+
+    shared = (([], []), ([], []))
+
     def turn(k):
         b_all(k).wait_recv()
         halves = ([], [])
@@ -399,41 +441,87 @@
             mixed = recv_b[k, :, r * wide : (r + 1) * wide].reshape(chans, cols).astype(F32)
             finish(0, i, mixed)
             for side, half in enumerate(project(1, i)):
-                halves[side].append(half.reshape(n, mine, cols))
+                halves[side].append(half.reshape(peers, 2, mine, cols))
         for side in range(2):
-            send_c[k, :, side] = jnp.concatenate(halves[side], axis=1).astype(BF16)
-        for p in others():
+            block = jnp.concatenate([half[:, 0] for half in halves[side]], axis=1)
+            send_c[k, :, side] = block.astype(BF16)
+            for r in range(0, rows // MIDDLE, 2):
+                upper, lower = halves[side][r][:, 1], halves[side][r + 1][:, 1]
+                for to, pair in enumerate(trade(upper, lower)):
+                    shared[side][to].append(pair)
+        for p in near_others():
             c_copy(k, p).start()
-        recv_c[k, me] = send_c[k, me]
-
-    def multiply_second():
+        recv_c[k, here] = send_c[k, here]
+        if (k + 1) % (MIDDLE // SHARED) == 0:
+            at = k * SHARED // MIDDLE
+            for side in range(2):
+                for to in range(2):
+                    block = jnp.concatenate(shared[side][to], axis=1)
+                    send_f[at, to * peers : (to + 1) * peers, side] = block.astype(BF16)
+                    shared[side][to].clear()
+            recv_f[at, me] = send_f[at, me]
+
+    def partial_products():
         span = rows // MIDDLE * mine
         for k in range(MIDDLE):
             c_all(k).wait_recv()
-            for q in range(n):
+            for q in range(peers):
                 at = q * rows * mine + k * span
                 fx_left[at : at + span] = recv_c[k, q, 0].astype(F32)
                 fx_right[at : at + span] = recv_c[k, q, 1].astype(F32)
         for c in range(mine):
-            at = pl.ds(c, n * rows, stride=mine)
+            at = pl.ds(c, peers * rows, stride=mine)
             a = fx_left[at, :].astype(BF16)
             b = fx_right[at, :].astype(BF16)
-            f_prod[at, :] = mm(a, b, ((0,), (0,)))
+            f_prod[pl.ds(c, n * rows, stride=mine), :] = mm(a, b, ((0,), (0,)))
         span = rows // LAST * mine
         for k in range(LAST):
             for p in range(n):
                 send_d[k, p] = f_prod[pl.ds(p * rows * mine + k * span, span), :].astype(BF16)
+            recv_d[k, me] = send_d[k, me]
+            if k == 0:
+                for p in others():
+                    d_copy(k, p).start()
+
+    def shared_products():
+        span = rows // SHARED * few
+        for k in range(SHARED):
+            f_all(k).wait_recv()
+            for q in range(n):
+                at = q * rows * few + k * span
+                fx_left[at : at + span] = recv_f[k, q, 0].astype(F32)
+                fx_right[at : at + span] = recv_f[k, q, 1].astype(F32)
+        for c in range(few):
+            at = pl.ds(c, n * rows, stride=few)
+            a = fx_left[at, :].astype(BF16)
+            b = fx_right[at, :].astype(BF16)
+            f_prod[at, :] = mm(a, b, ((0,), (0,)))
+        span = rows // LAST * few
+        for k in range(LAST):
+            for p in range(n):
+                send_g[k, p] = f_prod[pl.ds(p * rows * few + k * span, span), :].astype(BF16)
+            if k > 0:
+                for p in others():
+                    d_copy(k, p).start()
             for p in others():
-                d_copy(k, p).start()
-            recv_d[k, me] = send_d[k, me]
+                g_copy(k, p).start()
+            recv_g[k, me] = send_g[k, me]
 
     def close(k):
         d_all(k).wait_recv()
-        mixed_all = recv_d[k].astype(F32)
+        both = recv_d[k].astype(F32)
+        summed = both[:peers] + both[peers:]
+        g_all(k).wait_recv()
+        ends = recv_g[k].astype(F32)
+        tails = []
+        for r in range(0, rows // LAST, 2):
+            pair = ends[:, r * few : (r + 2) * few]
+            tails += trade(pair[:peers], pair[peers:])
         biases = []
         normed_rows = []
         for r, i in enumerate(chunk(k, LAST)):
-            finish(1, i, mixed_all[:, r * mine : (r + 1) * mine].reshape(chans, cols))
+            mixed = jnp.concatenate([summed[:, r * mine : (r + 1) * mine], tails[r]], axis=1)
+            finish(1, i, mixed.reshape(chans, cols))
             normed = normalize_t(zt[:, at_row(i)].astype(F32), gain_cols[4]).astype(BF16)
             normed_rows.append(normed)
             biases.append(mm(b_pad[...].astype(BF16), normed))
@@ -481,18 +569,24 @@
     multiply_first()
     for k in range(MIDDLE):
         turn(k)
+    for k in range(SHARED):
+        for p in others():
+            f_copy(k, p).start()
     for k in range(FIRST):
         a_all(k).wait_send()
     for k in range(MIDDLE):
         b_all(k).wait_send()
-    multiply_second()
+    partial_products()
+    shared_products()
     for k in range(MIDDLE):
         c_all(k).wait_send()
-    closed = [close(k) for k in range(LAST)]
+    for k in range(SHARED):
+        f_all(k).wait_send()
     for k in range(LAST):
-        attention_inputs(k, closed[k])
+        attention_inputs(k, close(k))
     for k in range(LAST):
         d_all(k).wait_send()
+        g_all(k).wait_send()
 
     for k in range(LAST):
         e_all(k).wait_recv()
@@ -536,12 +630,15 @@
     wide = chans // peers
     vm = pl.BlockSpec(memory_space=pltpu.VMEM)
     hbm = pl.BlockSpec(memory_space=pltpu.HBM)
-    phases = FIRST + 2 * MIDDLE + 2 * LAST
+    phases = FIRST + 2 * MIDDLE + SHARED + 3 * LAST
+    few = mine // 2
     first = pltpu.VMEM((FIRST, 2 * peers, rows // FIRST * wide, cols), BF16)
     first_in = pltpu.VMEM((FIRST, 2 * n, rows // FIRST * wide, cols), BF16)
     back = pltpu.VMEM((MIDDLE, peers, rows // MIDDLE * wide, cols), BF16)
-    second = pltpu.VMEM((MIDDLE, n, 2, rows // MIDDLE * mine, cols), BF16)
+    second = pltpu.VMEM((MIDDLE, peers, 2, rows // MIDDLE * mine, cols), BF16)
+    rest = pltpu.VMEM((SHARED, n, 2, rows // SHARED * few, cols), BF16)
     home = pltpu.VMEM((LAST, n, rows // LAST * mine, cols), BF16)
+    home_few = pltpu.VMEM((LAST, n, rows // LAST * few, cols), BF16)
     bias = pltpu.VMEM((LAST, heads * rows // LAST, cols), BF16)
     bias_in = pltpu.VMEM((LAST, n, heads * rows // LAST, cols), BF16)
 
@@ -587,8 +684,12 @@
             back,
             second,
             second,
+            rest,
+            rest,
             home,
             home,
+            home_few,
+            home_few,
             bias,
             bias_in,
             pltpu.SemaphoreType.DMA((phases,)),
@@ -620,7 +721,8 @@
         rows, cols, chans = pair_rep.shape
         fits = (
             mesh.shape["col"] == 1
-            and n % 2 == 0
+            and n & (n - 1) == 0
+            and n > 1
             and chans == n * GROUP
             and rows == GROUP
             and cols == n * rows

time: 53.8 us -> 51.1 us (0.950)
  Pallas kernels: 52.3 us -> 49.6 us
    pallas_call x1, Pallas kernels: 52.3 us -> 49.6 us  [fused(): pl.pallas_call(functools.partial(fused_kernel, n), out_shape=jax.ShapeDty...]
where the time goes in v4:
time: 51.1 us; the launch traced here: 50.9 us
  Pallas kernels  49.6 us (97%)
  local copies, waits for them, and re-layouts  0.71 us (1%)
  between operations  0.66 us (1%)
    pallas_call x1, Pallas kernels, fused(): pl.pallas_call(functools.partial(fused_kernel, n), out_shape=jax.ShapeDty...  49.6 us

profile of v4, /device:TPU:0, one launch (start us, length us, event | category | flops | bytes accessed | tf_op | source)
XLA Modules:
  0.0 50.9 jit_solution(4712652514504195629)
XLA Ops:
  0.7 49.6 %fused_pair.1 = bf16[8,128,128]{2,1,0:T(8,128)(2,1)S(1)} custom-call(bf16[8,128,128]{2,1,0:T(8,128)(2,1)} %pair_hbm.1, s32[1,128]{1,0:T(1,128)} %bitcast.4, s32[1]{0:T(128)S(6)} %copy.13.crop_ref, f32[2,128]{1,0:T(2,128)} %gain_hbm.1, bf16[2,128,640]{2,1,0:T(8,128)(2,1)} %proj_hbm.1, f32[2,128]{1,0:T(2,128)} %mgain_hbm.1, bf16[2,128,128]{2,1,0:T(8,128)(2,1)} %mout_hbm.1, ...), custom_call_target="tpu_custom_call" | custom-call | tf_op jit(solution)/shard_map/fused_pair/pallas_call | solution.py:648
  50.2 0.7 %copy.14 = bf16[8,128,128]{2,1,0:T(8,128)(2,1)} copy(bf16[8,128,128]{2,1,0:T(8,128)(2,1)S(1)} %fused_pair.1) | data formatting | bytes 524288

commit v5 on v4

--- a/solution.py
+++ b/solution.py
@@ -151,6 +151,8 @@
 MIDDLE = 4
 SHARED = 2
 LAST = 2
+MIXED = (15, 7, 11, 3, 14, 6, 10, 2, 13, 5, 9, 1, 12, 4, 8)
+PAIRED = (15, 3, 14, 2, 13, 1, 12, 7, 11, 6, 10, 5, 9, 4, 8)
 LOG2E = 1.4426950408889634
 
 
@@ -314,14 +316,8 @@
             at, place = at + place * bit, 2 * place
         return at
 
-    def others():
-        return [partner(s) for s in range(n - 1, 0, -1)]
-
-    def near_others():
-        return [partner(s) for s in range(peers - 1, 0, -1)]
-
-    def far_others():
-        return [partner(s) for s in range(n - 1, peers - 1, -1)]
+    def order(listed):
+        return listed if len(listed) == n - 1 else range(n - 1, 0, -1)
 
     def a_both(k, p):
         src = send_a.at[k, pl.ds(2 * lax.rem(p, peers), 2)]
@@ -389,10 +385,8 @@
                     ]
         if k == 0:
             pl.semaphore_wait(barrier, n - 1)
-        for p in far_others():
-            a_right(k, p).start()
-        for p in near_others():
-            a_both(k, p).start()
+        for s in order(MIXED):
+            (a_both if s < peers else a_right)(k, partner(s)).start()
         recv_a[k, pl.ds(2 * me, 2)] = send_a[k, pl.ds(2 * here, 2)]
 
     def multiply_first():
@@ -414,8 +408,8 @@
         for k in range(MIDDLE):
             for p in range(peers):
                 send_b[k, p] = f_prod[pl.ds(p * rows * wide + k * span, span), :].astype(BF16)
-            for p in near_others():
-                b_copy(k, p).start()
+            for s in range(peers - 1, 0, -1):
+                b_copy(k, partner(s)).start()
             recv_b[k, here] = send_b[k, here]
 
     def finish(u, i, mixed):
@@ -449,8 +443,8 @@
                 upper, lower = halves[side][r][:, 1], halves[side][r + 1][:, 1]
                 for to, pair in enumerate(trade(upper, lower)):
                     shared[side][to].append(pair)
-        for p in near_others():
-            c_copy(k, p).start()
+        for s in range(peers - 1, 0, -1):
+            c_copy(k, partner(s)).start()
         recv_c[k, here] = send_c[k, here]
         if (k + 1) % (MIDDLE // SHARED) == 0:
             at = k * SHARED // MIDDLE
@@ -480,8 +474,8 @@
                 send_d[k, p] = f_prod[pl.ds(p * rows * mine + k * span, span), :].astype(BF16)
             recv_d[k, me] = send_d[k, me]
             if k == 0:
-                for p in others():
-                    d_copy(k, p).start()
+                for s in range(n - 1, 0, -1):
+                    d_copy(k, partner(s)).start()
 
     def shared_products():
         span = rows // SHARED * few
@@ -501,10 +495,10 @@
             for p in range(n):
                 send_g[k, p] = f_prod[pl.ds(p * rows * few + k * span, span), :].astype(BF16)
             if k > 0:
-                for p in others():
-                    d_copy(k, p).start()
-            for p in others():
-                g_copy(k, p).start()
+                for s in range(n - 1, 0, -1):
+                    d_copy(k, partner(s)).start()
+            for s in range(n - 1, 0, -1):
+                g_copy(k, partner(s)).start()
             recv_g[k, me] = send_g[k, me]
 
     def close(k):
@@ -528,8 +522,8 @@
         send_e[k] = jnp.concatenate(
             [row[h : h + 1] for h in range(heads) for row in biases], axis=0
         ).astype(BF16)
-        for p in others():
-            e_copy(k, p).start()
+        for s in range(n - 1, 0, -1):
+            e_copy(k, partner(s)).start()
         recv_e[k, me] = send_e[k]
         return normed_rows
 
@@ -570,8 +564,8 @@
     for k in range(MIDDLE):
         turn(k)
     for k in range(SHARED):
-        for p in others():
-            f_copy(k, p).start()
+        for s in order(PAIRED):
+            f_copy(k, partner(s)).start()
     for k in range(FIRST):
         a_all(k).wait_send()
     for k in range(MIDDLE):
@@ -606,8 +600,7 @@
             total = scores[i, :, at] + b_full[:, at]
             e = jnp.exp2(total - jnp.max(total, axis=0, keepdims=True))
             inverse = 1.0 / jnp.sum(e, axis=0, keepdims=True)
-            w = (e * inverse).astype(BF16)
-            parts.append(mm(vmat[i, h * dim : (h + 1) * dim, :], w))
+            parts.append(mm(vmat[i, h * dim : (h + 1) * dim, :], e.astype(BF16)) * inverse)
         attended = jnp.concatenate(parts, axis=0)
         gated = (gmat[i] * attended).astype(BF16)
         result = mm(out_t[2], gated)
@@ -615,7 +608,7 @@
         out_ref[i] = jnp.transpose(zt[:, at].astype(F32) + result).astype(BF16)
         return carry
 
-    lax.fori_loop(0, rows, attend, 0, unroll=4)
+    lax.fori_loop(0, rows, attend, 0, unroll=8)
 
     for k in range(LAST):
         e_all(k).wait_send()

time: 51.1 us -> 50.1 us (0.980)
  Pallas kernels: 49.6 us -> 48.6 us
    pallas_call x1, Pallas kernels: 49.6 us -> 48.6 us  [fused(): pl.pallas_call(functools.partial(fused_kernel, n), out_shape=jax.ShapeDty...]
where the time goes in v5:
time: 50.1 us; the launch traced here: 49.9 us
  Pallas kernels  48.6 us (97%)
  local copies, waits for them, and re-layouts  0.71 us (1%)
  between operations  0.66 us (1%)
    pallas_call x1, Pallas kernels, fused(): pl.pallas_call(functools.partial(fused_kernel, n), out_shape=jax.ShapeDty...  48.6 us

profile of v5, /device:TPU:0, one launch (start us, length us, event | category | flops | bytes accessed | tf_op | source)
XLA Modules:
  0.0 49.9 jit_solution(5919261002439522127)
XLA Ops:
  0.7 48.6 %fused_pair.1 = bf16[8,128,128]{2,1,0:T(8,128)(2,1)S(1)} custom-call(bf16[8,128,128]{2,1,0:T(8,128)(2,1)} %pair_hbm.1, s32[1,128]{1,0:T(1,128)} %bitcast.4, s32[1]{0:T(128)S(6)} %copy.13.crop_ref, f32[2,128]{1,0:T(2,128)} %gain_hbm.1, bf16[2,128,640]{2,1,0:T(8,128)(2,1)} %proj_hbm.1, f32[2,128]{1,0:T(2,128)} %mgain_hbm.1, bf16[2,128,128]{2,1,0:T(8,128)(2,1)} %mout_hbm.1, ...), custom_call_target="tpu_custom_call" | custom-call | tf_op jit(solution)/shard_map/fused_pair/pallas_call | solution.py:641
  49.2 0.7 %copy.14 = bf16[8,128,128]{2,1,0:T(8,128)(2,1)} copy(bf16[8,128,128]{2,1,0:T(8,128)(2,1)S(1)} %fused_pair.1) | data formatting | bytes 524288

commit v6 on v5

--- a/solution.py
+++ b/solution.py
@@ -247,6 +247,7 @@
     d_phase = f_phase + SHARED
     g_phase = d_phase + LAST
     e_phase = g_phase + LAST
+    a_phase = e_phase + LAST
     few = mine // 2
 
     barrier = pltpu.get_barrier_semaphore()
@@ -324,11 +325,17 @@
         return remote(k, src, recv_a.at[k, pl.ds(2 * me, 2)], p)
 
     def a_right(k, p):
-        return remote(k, send_a.at[k, 2 * lax.rem(p, peers) + 1], recv_a.at[k, 2 * me + 1], p)
-
-    def a_all(k):
-        block = recv_a.at[k, : 2 * (peers - 1) + peers]
+        return remote(
+            a_phase + k, send_a.at[k, 2 * lax.rem(p, peers) + 1], recv_a.at[k, 2 * me + 1], p
+        )
+
+    def a_near(k):
+        block = recv_a.at[k, : 2 * (peers - 1)]
         return remote(k, block, block, me)
+
+    def a_far(k):
+        block = recv_a.at[k, :peers]
+        return remote(a_phase + k, block, block, me)
 
     def b_copy(k, p):
         return remote(FIRST + k, send_b.at[k, lax.rem(p, peers)], recv_b.at[k, here], p)
@@ -369,11 +376,15 @@
 
     def project(u, i):
         normed = normalize_t(zt[:, at_row(i)].astype(F32), gain_cols[u]).astype(BF16)
-        pr = mm(proj_t[u], normed)
+        pr = mm(proj_t[u, : 4 * hid], normed)
         left = masks[i] * sigmoid(pr[hid : 2 * hid]) * pr[:hid]
         right = masks[i] * sigmoid(pr[3 * hid : 4 * hid]) * pr[2 * hid : 3 * hid]
-        og[:, at_row(i)] = sigmoid(pr[4 * hid :])
         return left, right
+
+    def gates(u):
+        for i in range(rows):
+            normed = normalize_t(zt[:, at_row(i)].astype(F32), gain_cols[u]).astype(BF16)
+            og[:, at_row(i)] = sigmoid(mm(proj_t[u, 4 * hid :], normed))
 
     def start_first(k):
         for r, i in enumerate(chunk(k, FIRST)):
@@ -392,13 +403,16 @@
     def multiply_first():
         span = rows // FIRST * wide
         for k in range(FIRST):
-            a_all(k).wait_recv()
+            a_far(k).wait_recv()
+            for q in range(peers):
+                at = pl.multiple_of((far + q) * rows * wide + k * span, span)
+                fx_right[pl.ds(at, span)] = recv_a[k, 2 * (far + q) + 1].astype(F32)
+            a_near(k).wait_recv()
             for q in range(peers):
                 at = q * rows * wide + k * span
                 fx_left[at : at + span] = recv_a[k, 2 * (near + q)].astype(F32)
-            for q in range(n):
-                at = q * rows * wide + k * span
-                fx_right[at : at + span] = recv_a[k, 2 * q + 1].astype(F32)
+                at = pl.multiple_of((near + q) * rows * wide + k * span, span)
+                fx_right[pl.ds(at, span)] = recv_a[k, 2 * (near + q) + 1].astype(F32)
         for c in range(wide):
             at = pl.ds(c, peers * rows, stride=wide)
             a = fx_left[at, :].astype(BF16)
@@ -539,13 +553,15 @@
             scores[i] = mm(kmat[i], q_heads[i]) * (LOG2E / float(dim) ** 0.5)
 
     gain_cols[0] = column(gain_ref[0:1, :])
-    proj_t[0] = flip(proj_ref[0])
+    proj_t[0, : 4 * hid] = flip(proj_ref[0, :, : 4 * hid])
     for i in range(rows):
         zt[:, at_row(i)] = flip(pair_ref[i])
     for k in range(FIRST):
         start_first(k)
     for load in loads[4:]:
         load.wait()
+    proj_t[0, 4 * hid :] = flip(proj_ref[0, :, 4 * hid :])
+    gates(0)
     gain_cols[1] = column(gain_ref[1:2, :])
     gain_cols[2] = column(mgain_ref[0:1, :])
     gain_cols[3] = column(mgain_ref[1:2, :])
@@ -566,8 +582,10 @@
     for k in range(SHARED):
         for s in order(PAIRED):
             f_copy(k, partner(s)).start()
+    gates(1)
     for k in range(FIRST):
-        a_all(k).wait_send()
+        a_near(k).wait_send()
+        a_far(k).wait_send()
     for k in range(MIDDLE):
         b_all(k).wait_send()
     partial_products()
@@ -623,7 +641,7 @@
     wide = chans // peers
     vm = pl.BlockSpec(memory_space=pltpu.VMEM)
     hbm = pl.BlockSpec(memory_space=pltpu.HBM)
-    phases = FIRST + 2 * MIDDLE + SHARED + 3 * LAST
+    phases = 2 * FIRST + 2 * MIDDLE + SHARED + 3 * LAST
     few = mine // 2
     first = pltpu.VMEM((FIRST, 2 * peers, rows // FIRST * wide, cols), BF16)
     first_in = pltpu.VMEM((FIRST, 2 * n, rows // FIRST * wide, cols), BF16)

time: 50.1 us -> 50 us (level)
  no operation moved by 1% of the time
where the time goes in v6:
time: 50 us; the launch traced here: 49.9 us
  Pallas kernels  48.5 us (97%)
  local copies, waits for them, and re-layouts  0.71 us (1%)
  between operations  0.66 us (1%)
    pallas_call x1, Pallas kernels, fused(): pl.pallas_call(functools.partial(fused_kernel, n), out_shape=jax.ShapeDty...  48.5 us

profile of v6, /device:TPU:0, one launch (start us, length us, event | category | flops | bytes accessed | tf_op | source)
XLA Modules:
  0.0 49.9 jit_solution(11531071873318146491)
XLA Ops:
  0.7 48.5 %fused_pair.1 = bf16[8,128,128]{2,1,0:T(8,128)(2,1)S(1)} custom-call(bf16[8,128,128]{2,1,0:T(8,128)(2,1)} %pair_hbm.1, s32[1,128]{1,0:T(1,128)} %bitcast.4, s32[1]{0:T(128)S(6)} %copy.13.crop_ref, f32[2,128]{1,0:T(2,128)} %gain_hbm.1, bf16[2,128,640]{2,1,0:T(8,128)(2,1)} %proj_hbm.1, f32[2,128]{1,0:T(2,128)} %mgain_hbm.1, bf16[2,128,128]{2,1,0:T(8,128)(2,1)} %mout_hbm.1, ...), custom_call_target="tpu_custom_call" | custom-call | tf_op jit(solution)/shard_map/fused_pair/pallas_call | solution.py:659
  49.2 0.7 %copy.14 = bf16[8,128,128]{2,1,0:T(8,128)(2,1)} copy(bf16[8,128,128]{2,1,0:T(8,128)(2,1)S(1)} %fused_pair.1) | data formatting | bytes 524288
